TPU v7x, 32 devices: a whole 2x2x4 slice. The times are simulated.
32 devices in a mesh: chol: 16 (over z, x, core), virt: 2 (over y).
Axes of the slice: x: 2, y: 2, z: 4, core: 2. Of those that a mesh axis runs over, the one named last changes fastest.
Arguments:
- amplitudes: bfloat16 [9600, 600], P('chol'), may hold values from -6 to 6
- chol_vectors: bfloat16 [128, 600, 600], P('chol', 'virt'), may hold values from -0.072753906 to 0.072753906
Outputs:
- sigma: float32 [9600, 600], P('chol', 'virt')
All inputs are finite; a program needn't handle non-finite values.
Results may differ from a plain program's by a relative error of at most 0.0042.
Values may be sent and summed in bfloat16 or wider, within the bound.
A program may use at most 192 MiB of HBM per device.

v0:
```python
import jax
import jax.numpy as jnp
from jax import lax
from jax.sharding import PartitionSpec as P


def shards(amplitudes, chol_vectors):
    vec_count, row_share, orbitals = chol_vectors.shape
    turned = jnp.transpose(chol_vectors, (1, 2, 0)).reshape(row_share, orbitals * vec_count)
    local_flat = chol_vectors.reshape(vec_count * row_share, orbitals)
    ladder_half = jnp.dot(
        lax.all_gather(amplitudes, "chol", axis=0, tiled=True),
        local_flat.T,
        preferred_element_type=jnp.float32,
    ).astype(jnp.bfloat16)
    combos = ladder_half.shape[0] // orbitals
    half_blocks = ladder_half.reshape(combos, orbitals * vec_count, row_share)
    sigma_terms = jnp.einsum(
        "ak,nkb->nab",
        lax.all_gather(turned, "virt", axis=0, tiled=True),
        half_blocks,
        preferred_element_type=jnp.float32,
    )
    sigma_terms = sigma_terms.reshape(combos * orbitals, row_share)
    return lax.psum_scatter(sigma_terms, "chol", scatter_dimension=0, tiled=True)


def solution(mesh):
    placed = (P("chol", None), P("chol", "virt", None))
    return jax.shard_map(
        shards, mesh=mesh, in_specs=placed, out_specs=P("chol", "virt"), check_vma=False
    )
```

profile of v0, /device:TPU:0, one launch (start us, length us, event | category | flops | bytes accessed | tf_op | source)
XLA Modules:
  0.0 710.1 jit_solution(12866247792916861273)
XLA Ops:
  6.5 0.0 all-gather.6.cloned.1.call-start
  6.5 6.3 copy.11
  12.9 5.7 copy.12
  18.5 0.0 all-gather.6.cloned.1.call-update
  18.5 0.0 all-gather.4.cloned.1.call-start
  18.6 0.7 all-gather.4.cloned.1.call-update
  19.3 0.0 all-reduce.3.cloned.1.call-start
  19.3 2.3 copy.9
  21.6 2.7 reshape.12
  24.3 0.0 copy-start
  24.3 73.2 %all-gather.6.cloned.1.call-done = bf16[2,300,4800]{2,1,0:T(8,128)(2,1)} async-done(((bf16[1,300,4800]{2,1,0:T(8,128)(2,1)}), bf16[2,300,4800]{2,1,0:T(8,128)(2,1)}) %all-gather.6.cloned.1.call-update) | async-done | bytes 5760016 | tf_op jit(solution)/shard_map/all_gather | solution.py:20
  97.5 7.7 %reshape.19 = bf16[600,4800,1]{1,0,2:T(8,128)(2,1)} reshape(bf16[2,300,4800]{2,1,0:T(8,128)(2,1)} %all-gather.6.cloned.1.call-done) | data formatting | bytes 11520000
  105.2 93.1 %all-gather.4.cloned.1.call-done = bf16[9600,600]{1,0:T(8,128)(2,1)} async-done(((bf16[600,600]{1,0:T(8,128)(2,1)}), bf16[9600,600]{1,0:T(8,128)(2,1)}) %all-gather.4.cloned.1.call-update) | async-done | bytes 11520016 | tf_op jit(solution)/shard_map/all_gather | solution.py:12
  198.3 0.0 copy-done
  198.3 45.2 %convolution_convert_fusion = bf16[9600,2400]{0,1:T(8,128)(2,1)} fusion(bf16[9600,600]{1,0:T(8,128)(2,1)} %all-gather.4.cloned.1.call-done, bf16[2400,600]{1,0:T(8,128)(2,1)S(1)} %copy-done), kind=kOutput, calls=%fused_computation | convolution fusion | flops 27671040000 | bytes 60480000 | tf_op jit(solution)/shard_map/dot_general | solution.py:11
  243.6 57.3 %copy.10 = bf16[9600,2400]{1,0:T(8,128)(2,1)} copy(bf16[9600,2400]{0,1:T(8,128)(2,1)} %convolution_convert_fusion) | data formatting | bytes 92160000 | tf_op jit(solution)/shard_map/convert_element_type | solution.py:15
  300.9 101.2 %reshape.13 = bf16[16,4800,300]{2,1,0:T(8,128)(2,1)} reshape(bf16[9600,2400]{1,0:T(8,128)(2,1)} %copy.10) | data formatting | bytes 92160000 | tf_op jit(solution)/shard_map/reshape | solution.py:17
  402.1 54.4 %convolution_bitcast_fusion = f32[16,600,300]{1,2,0:T(8,128)} fusion(bf16[16,4800,300]{2,1,0:T(8,128)(2,1)} %reshape.13, bf16[600,4800,1]{1,0,2:T(8,128)(2,1)} %reshape.19), kind=kOutput, calls=%fused_computation.1 | convolution fusion | flops 27648000000 | bytes 63360000 | tf_op jit(solution)/shard_map/ak,nkb->nab/dot_general | solution.py:18
  456.4 13.0 %copy.14 = f32[16,600,300]{1,0,2:T(8,128)} copy(f32[16,600,300]{1,2,0:T(8,128)} %convolution_bitcast_fusion) | data formatting | bytes 23040000 | tf_op jit(solution)/shard_map/ak,nkb->nab/transpose | solution.py:18
  469.4 14.1 %reshape.15 = f32[9600,300]{0,1:T(8,128)} reshape(f32[16,600,300]{1,0,2:T(8,128)} %copy.14) | data formatting | bytes 23040000 | tf_op jit(solution)/shard_map/reshape | solution.py:24
  483.5 0.0 copy-start.1
  483.5 0.0 all-reduce.3.cloned.1.call-update
  483.5 0.6 copy-done.1
  484.2 0.6 dynamic-slice
  485.4 215.8 %all-reduce.3.cloned.1.call-done = f32[9600,300]{0,1:T(8,128)} async-done(((f32[9600,300]{0,1:T(8,128)}), f32[9600,300]{0,1:T(8,128)}) %all-reduce.3.cloned.1.call-update) | async-done | bytes 11520016
  701.2 2.3 constant_dynamic-slice_fusion
Async XLA Ops:
  6.5 91.0 %all-gather.6.cloned.1.call-start = ((), (), s32[]{:S(2)}) async-start(), calls=%async_computation.1 | async-start | bytes 8871936 | tf_op jit(solution)/shard_map/all_gather | solution.py:20
  18.5 179.8 %all-gather.4.cloned.1.call-start = ((), (), s32[]{:S(2)}) async-start(), calls=%async_computation | async-start | bytes 13056000 | tf_op jit(solution)/shard_map/all_gather | solution.py:12
  19.3 681.9 %all-reduce.3.cloned.1.call-start = ((), (), s32[]{:S(2)}) async-start(), calls=%async_computation.2 | async-start | bytes 23347200
  24.3 174.0 %copy-start = (bf16[2400,600]{1,0:T(8,128)(2,1)S(1)}, bf16[2400,600]{1,0:T(8,128)(2,1)}, u32[]{:S(2)}) copy-start(bf16[2400,600]{1,0:T(8,128)(2,1)} %reshape.12) | copy-start | bytes 8640004
  483.5 0.7 copy-start.1
Sparse Core Ops, SparseCore 0:
  18.7 78.8 all-gather.5
  99.7 98.6 all-gather.3
  483.7 217.5 all-reduce.2
where the time goes:
time: 715 us; the launch traced here: 710 us
  waiting for transfers between devices  383 us (54%)
  local copies, waits for them, and re-layouts  214 us (30%)
  matrix products  99.6 us (14%)
  between operations  13.8 us (2%)
    unnamed x4, waiting for transfers between devices  217 us
    reshape x1, local copies, waits for them, and re-layouts, shards(): half_blocks = ladder_half.reshape(combos, orbitals * vec_count, row_share)  101 us
    all_gather x1, waiting for transfers between devices, shards(): lax.all_gather(amplitudes, 'chol', axis=0, tiled=True)  93.1 us
    all_gather x1, waiting for transfers between devices, shards(): lax.all_gather(turned, 'virt', axis=0, tiled=True)  73.2 us
    convert_element_type x1, local copies, waits for them, and re-layouts, shards(): ladder_half = jnp.dot(lax.all_gather(amplitudes, 'chol', axis=0, tiled=Tr...  57.3 us
    dot_general x1, matrix products, shards(): jnp.einsum('ak,nkb->nab', lax.all_gather(turned, 'virt', axis=0, tiled=Tr...  54.4 us
    dot_general x1, matrix products, shards(): jnp.dot(lax.all_gather(amplitudes, 'chol', axis=0, tiled=True), local_fla...  45.2 us
    unnamed x9, local copies, waits for them, and re-layouts  19.2 us
  transfers between devices with their start and end apart: 3, of which 3 were waited for; matrix products, arithmetic and copies ran while one was open for 2% of the time, Pallas kernels for 0%

commit v1 on v0

--- a/solution.py
+++ b/solution.py
@@ -1,10 +1,21 @@
+import functools
+
 import jax
 import jax.numpy as jnp
 from jax import lax
+from jax.experimental import pallas as pl
+from jax.experimental.pallas import tpu as pltpu
 from jax.sharding import PartitionSpec as P
 
-
-def shards(amplitudes, chol_vectors):
+MESH = pl.DeviceIdType.MESH
+KEPT = 4
+
+
+def up(size, unit):
+    return -(-size // unit) * unit
+
+
+def plain(amplitudes, chol_vectors):
     vec_count, row_share, orbitals = chol_vectors.shape
     turned = jnp.transpose(chol_vectors, (1, 2, 0)).reshape(row_share, orbitals * vec_count)
     local_flat = chol_vectors.reshape(vec_count * row_share, orbitals)
@@ -25,7 +36,196 @@
     return lax.psum_scatter(sigma_terms, "chol", scatter_dimension=0, tiled=True)
 
 
+def kernel(ring, r_in, l_in, out, rbuf, lbuf, xbuf, xtmp, acc, sendbuf, recvbuf,
+           loc_sem, r_send, r_recv, d_send, d_recv, y_send, y_recv, f_send, f_recv,
+           p_send, p_recv):
+    half = ring // 2
+    chol, virt = lax.axis_index("chol"), lax.axis_index("virt")
+    core, chip = chol % 2, chol // 2
+    odd = chip % 2
+    pos = (1 - odd) * (chip // 2) + odd * (ring - 1 - chip // 2)
+    vecs, rows, width = l_in.shape
+    tall = r_in.shape[0]
+
+    def at(offset):
+        there = (pos + offset + ring) % ring
+        back = there // half
+        q = (1 - back) * 2 * there + back * (2 * (ring - 1 - there) + 1)
+        return (q * 2 + core, virt)
+
+    partner, across = (chip * 2 + 1 - core, virt), (chol, 1 - virt)
+
+    barrier = pltpu.get_barrier_semaphore()
+    for peer in [at(r) for r in range(1, ring)] + [partner, across]:
+        pl.semaphore_signal(barrier, inc=1, device_id=peer, device_id_type=MESH)
+
+    cp_r = pltpu.make_async_copy(r_in, rbuf.at[0, pl.ds(0, tall)], loc_sem.at[0])
+    cp_l = pltpu.make_async_copy(l_in, lbuf.at[virt, core], loc_sem.at[1])
+    cp_r.start()
+    cp_l.start()
+    if width > tall:
+        rbuf[:, tall:, :] = jnp.zeros((ring, width - tall, width), rbuf.dtype)
+    cp_r.wait()
+    cp_l.wait()
+    pl.semaphore_wait(barrier, ring + 1)
+
+    def remote(src, dst, s, r, to):
+        return pltpu.make_async_remote_copy(
+            src_ref=src, dst_ref=dst, send_sem=s, recv_sem=r, device_id=to, device_id_type=MESH)
+
+    def hop_up(d):
+        return remote(rbuf.at[d - 1, pl.ds(0, tall)], rbuf.at[d, pl.ds(0, tall)],
+                      r_send.at[d], r_recv.at[d], at(1))
+
+    def hop_down(d):
+        src = 0 if d == ring - 1 else d + 1
+        return remote(rbuf.at[src, pl.ds(0, tall)], rbuf.at[d, pl.ds(0, tall)],
+                      r_send.at[d], r_recv.at[d], at(-1))
+
+    hops = {d: hop_up(d) for d in range(1, half + 1)}
+    hops.update({d: hop_down(d) for d in range(half + 1, ring)})
+    give = remote(lbuf.at[virt, core], lbuf.at[virt, core], d_send, d_recv, partner)
+    cross = [remote(lbuf.at[virt, core, j], lbuf.at[virt, core, j], y_send.at[j], y_recv.at[j], across)
+             for j in range(vecs)]
+    share = [remote(lbuf.at[1 - virt, core, j], lbuf.at[1 - virt, core, j], f_send.at[j], f_recv.at[j], partner)
+             for j in range(vecs)]
+
+    hops[1].start()
+    hops[ring - 1].start()
+    for c in cross:
+        c.start()
+    give.start()
+
+    part = vecs // 2
+    chunk = part * rows
+
+    def stage_one(slot, c, j, dst, first):
+        left = lbuf[virt, c, pl.ds(j * part, part)].reshape(chunk, width)
+        dst[pl.ds(first, chunk), :] = lax.dot_general(
+            left, rbuf[slot], (((1,), (1,)), ((), ())),
+            preferred_element_type=jnp.float32).astype(jnp.bfloat16)
+
+    def keep(slot, k):
+        @pl.loop(0, 4)
+        def _(i):
+            stage_one(slot, i // 2, i % 2, xbuf.at[k], pl.multiple_of(i * chunk, chunk))
+
+    give.wait_recv()
+    keep(0, 0)
+    kept = {0: 0}
+    moved = 0
+    for s in range(1, half + 1):
+        due = [s] if s == half else [s, ring - s]
+        for d in due:
+            hops[d].wait_recv()
+        if s < half:
+            hops[s + 1].start()
+            if ring - s - 1 > half:
+                hops[ring - s - 1].start()
+        goal = (vecs * s) // half
+        for j in range(moved, goal):
+            cross[j].wait_recv()
+            share[j].start()
+        moved = goal
+        for d in due:
+            if len(kept) < KEPT:
+                kept[d] = len(kept)
+                keep(d, kept[d])
+    for j in range(vecs):
+        share[j].wait_recv()
+
+    def second(p, x0, x1):
+        both = jnp.concatenate([x0, x1], axis=0)
+        c, j = p // vecs, p % vecs
+        weights = jnp.concatenate([lbuf[0, c, j], lbuf[1, c, j]], axis=0)
+        acc[...] += lax.dot_general(both, weights, (((1,), (1,)), ((), ())),
+                                    preferred_element_type=jnp.float32)
+
+    far = sorted((d for d in range(ring) if d not in kept), key=lambda d: -min(d, ring - d))
+    near = sorted(kept, key=lambda d: -min(d, ring - d))
+    order = far + near
+    posts = []
+    for g in range(0, ring, 2):
+        pair = order[g:g + 2]
+        acc[...] = jnp.zeros_like(acc)
+        if pair[0] in kept:
+            @pl.loop(0, 2 * vecs)
+            def _(p):
+                first = pl.ds(pl.multiple_of(p * rows, rows), rows)
+                second(p, xbuf[kept[pair[0]], first, :], xbuf[kept[pair[1]], first, :])
+        else:
+            @pl.loop(0, 4)
+            def _(i):
+                for t in range(2):
+                    stage_one(pair[t], i // 2, i % 2, xtmp.at[t], 0)
+
+                @pl.loop(0, part)
+                def _(m):
+                    first = pl.ds(pl.multiple_of(m * rows, rows), rows)
+                    second(i * part + m, xtmp[0, first, :], xtmp[1, first, :])
+        for t in range(2):
+            d = pair[t]
+            if d == 0:
+                out[...] = acc[pl.ds(t * rows, rows), :]
+            else:
+                sendbuf[d - 1] = acc[pl.ds(t * rows, rows), :].astype(jnp.bfloat16)
+                post = remote(sendbuf.at[d - 1], recvbuf.at[d - 1], p_send.at[d - 1], p_recv.at[d - 1], at(-d))
+                post.start()
+                posts.append((d, post))
+    for d, post in posts:
+        post.wait_recv()
+        out[...] += recvbuf[d - 1].astype(jnp.float32)
+    for d, post in posts:
+        post.wait_send()
+    for d in hops:
+        hops[d].wait_send()
+    for c in cross + share:
+        c.wait_send()
+    give.wait_send()
+
+
+def fused(ring, amplitudes, chol_vectors):
+    vecs, share, orbitals = chol_vectors.shape
+    rows, width, tall = up(share, 16), up(orbitals, 128), up(orbitals, 16)
+    bf, f32 = jnp.bfloat16, jnp.float32
+    r = jnp.pad(amplitudes, ((0, tall - orbitals), (0, width - orbitals)))
+    l = jnp.pad(chol_vectors, ((0, 0), (0, rows - share), (0, width - orbitals)))
+    dma = pltpu.SemaphoreType.DMA
+    turned = pl.pallas_call(
+        functools.partial(kernel, ring),
+        out_shape=jax.ShapeDtypeStruct((rows, 2 * rows), f32),
+        in_specs=[pl.BlockSpec(memory_space=pl.ANY)] * 2,
+        out_specs=pl.BlockSpec(memory_space=pltpu.VMEM),
+        scratch_shapes=[
+            pltpu.VMEM((ring, width, width), bf),
+            pltpu.VMEM((2, 2, vecs, rows, width), bf),
+            pltpu.VMEM((KEPT, 2 * vecs * rows, width), bf),
+            pltpu.VMEM((2, vecs // 2 * rows, width), bf),
+            pltpu.VMEM((2 * rows, 2 * rows), f32),
+            pltpu.VMEM((ring - 1, rows, 2 * rows), bf),
+            pltpu.VMEM((ring - 1, rows, 2 * rows), bf),
+            dma((2,)), dma((ring,)), dma((ring,)), dma, dma,
+            dma((vecs,)), dma((vecs,)), dma((vecs,)), dma((vecs,)),
+            dma((ring - 1,)), dma((ring - 1,)),
+        ],
+        compiler_params=pltpu.CompilerParams(
+            collective_id=0, has_side_effects=True, vmem_limit_bytes=67043328),
+        name="ladder",
+    )(r, l)
+    sides = jnp.concatenate([turned[:share, :share], turned[:share, rows:rows + share]], axis=1)
+    return sides.T
+
+
 def solution(mesh):
+    chol, virt = mesh.shape["chol"], mesh.shape["virt"]
+
+    def shards(amplitudes, chol_vectors):
+        vecs, share, orbitals = chol_vectors.shape
+        fits = virt == 2 and chol % 4 == 0 and chol >= 16 and vecs % 2 == 0
+        if fits and amplitudes.shape[0] == orbitals:
+            return fused(chol // 2, amplitudes, chol_vectors)
+        return plain(amplitudes, chol_vectors)
+
     placed = (P("chol", None), P("chol", "virt", None))
     return jax.shard_map(
         shards, mesh=mesh, in_specs=placed, out_specs=P("chol", "virt"), check_vma=False

time: 715 us -> 181 us (0.25)
  waiting for transfers between devices: 383 us -> 0 us
  local copies, waits for them, and re-layouts: 214 us -> 6.51 us
  Pallas kernels: 0 us -> 173 us
  matrix products: 99.6 us -> 0 us
  between operations: 13.8 us -> 0.02 us
    unnamed x4 -> x0, waiting for transfers between devices: 217 us -> none
    pallas_call x0 -> x1, Pallas kernels: none -> 173 us  [fused(): pl.pallas_call(functools.partial(kernel, ring), out_shape=jax.ShapeDtypeS...]
    all_gather x2 -> x0, waiting for transfers between devices: 166 us -> none  [the longest x1 93.1 us: shards(): lax.all_gather(amplitudes, 'chol', axis=0, tiled=True)]
    reshape x3 -> x0, local copies, waits for them, and re-layouts: 118 us -> none  [the longest x1 101 us: shards(): half_blocks = ladder_half.reshape(combos, orbitals * vec_count, row_share)]
    dot_general x2 -> x0, matrix products: 99.6 us -> none  [the longest x1 54.4 us: shards(): jnp.einsum('ak,nkb->nab', lax.all_gather(turned, 'virt', axis=0, tiled=Tr...]
    convert_element_type x1 -> x0, local copies, waits for them, and re-layouts: 57.3 us -> none  [shards(): ladder_half = jnp.dot(lax.all_gather(amplitudes, 'chol', axis=0, tiled=Tr...]
    transpose x2 -> x0, local copies, waits for them, and re-layouts: 19.3 us -> none  [the longest x1 13 us: shards(): jnp.einsum('ak,nkb->nab', lax.all_gather(turned, 'virt', axis=0, tiled=Tr...]
    unnamed x9 -> x3, local copies, waits for them, and re-layouts: 19.2 us -> 2.27 us
  transfers between devices with their start and end apart: 3 -> 0, of which waited for: 3 -> 0; matrix products, arithmetic and copies ran while one was open for 2% -> 0% of each run, Pallas kernels for 0% -> 0%
where the time goes in v1:
time: 181 us
  Pallas kernels  173 us (96%)
  local copies, waits for them, and re-layouts  6.51 us (4%)
    pallas_call x1, Pallas kernels, fused(): pl.pallas_call(functools.partial(kernel, ring), out_shape=jax.ShapeDtypeS...  173 us

profile of v1, /device:TPU:0, one launch (start us, length us, event | category | flops | bytes accessed | tf_op | source)
XLA Modules:
  0.0 180.7 jit_solution(17695934033060782374)
XLA Ops:
  0.0 2.3 %copy.3 = bf16[8,300,600]{2,1,0:T(8,128)(2,1)S(1)} copy(bf16[8,300,600]{2,0,1:T(8,128)(2,1)} %param.3) | data formatting | bytes 5760000 | tf_op args[1]
  2.3 0.0 copy-start
  2.3 1.9 %pad.9.l_in = bf16[8,304,640]{2,1,0:T(8,128)(2,1)} pad(bf16[8,300,600]{2,1,0:T(8,128)(2,1)S(1)} %copy.3, bf16[]{:T(256)} %constant.2.clone.1), padding=0_0x0_4x0_40 | pad | bytes 5992962 | tf_op jit(solution)/shard_map/jit(_pad)/pad | solution.py:192
  4.2 0.0 copy-done
  4.2 0.9 pad.8.r_in
  5.2 173.1 %ladder.1 = f32[304,608]{1,0:T(8,128)} custom-call(bf16[608,640]{1,0:T(8,128)(2,1)} %pad.8.r_in, bf16[8,304,640]{2,1,0:T(8,128)(2,1)} %pad.9.l_in), custom_call_target="tpu_custom_call" | custom-call | tf_op jit(solution)/shard_map/ladder/pallas_call | solution.py:194
  178.3 1.3 fusion
  179.6 1.1 maximum_bitcast_fusion
Async XLA Ops:
  2.3 2.0 %copy-start = (bf16[600,600]{1,0:T(8,128)(2,1)S(1)}, bf16[600,600]{1,0:T(8,128)(2,1)}, u32[]{:S(2)}) copy-start(bf16[600,600]{1,0:T(8,128)(2,1)} %param.2) | copy-start | bytes 2160004
